TPU v7x, 32 devices: a whole 2x2x4 slice. The times are simulated.
32 devices in a mesh: ep: 8 (over z, x), tp: 4 (over y, core).
Axes of the slice: x: 2, y: 2, z: 4, core: 2. Of those that a mesh axis runs over, the one named last changes fastest.
Arguments:
- tokens: bfloat16 [2048, 2880], P('ep', 'tp'), may hold values from -6 to 6
- expert_ids: int32 [2048, 4], P('ep'), may hold values from 0 to 15, all different within a row; in each aligned block of 256 rows (0 to 255, 256 to 511, ...) at most 128 rows name the same one
- combine_weights: float32 [2048, 4], P('ep'), may hold values from 0.05 to 0.6
- gate_weight: bfloat16 [16, 2880, 2880], P('ep', None, 'tp'), may hold values from -0.109375 to 0.109375
- up_weight: bfloat16 [16, 2880, 2880], P('ep', None, 'tp'), may hold values from -0.109375 to 0.109375
- down_weight: bfloat16 [16, 2880, 2880], P('ep', 'tp'), may hold values from -0.109375 to 0.109375
Outputs:
- mixed: bfloat16 [2048, 2880], P('ep', 'tp')
Inputs may be any that keep to these rules, and one draw needn't show every extreme that they name: `expert_ids`: each row names 4 different experts; within the 256 rows of one index of ep no expert is named more than 128 times, a bound that some block reaches.
All inputs are finite; a program needn't handle non-finite values.
Results may differ from a plain program's by a relative error of at most 0.014.
Values may be sent and summed in bfloat16 or wider, within the bound.
A program may use at most 128 MiB of HBM per device.

v0:
```python
import jax
import jax.numpy as jnp
from jax import lax
from jax.sharding import PartitionSpec as P


def activate(gate_acc, up_acc):
    return (up_acc + 1.0) * gate_acc * jax.nn.sigmoid(1.702 * gate_acc)


def local(tokens, expert_ids, combine_weights, gate_weight, up_weight, down_weight):
    ep_count = lax.axis_size("ep")
    exp_local = gate_weight.shape[0]
    experts = exp_local * ep_count
    tok_rows = expert_ids.shape[0]
    top_count = expert_ids.shape[1]
    capacity = 2 * tok_rows * top_count // experts
    feat_width = tokens.shape[1]
    flat_ids = expert_ids.reshape(-1)
    onehot = (flat_ids[:, None] == jnp.arange(experts, dtype=jnp.int32)[None, :]).astype(jnp.int32)
    slot_pos = jnp.sum((jnp.cumsum(onehot, axis=0) - onehot) * onehot, axis=1)
    expert_local = flat_ids % exp_local
    owner_dev = flat_ids // exp_local
    token_of = jnp.arange(tok_rows * top_count, dtype=jnp.int32) // top_count
    send_buf = jnp.zeros((exp_local, ep_count, capacity, feat_width), jnp.bfloat16)
    send_buf = send_buf.at[expert_local, owner_dev, slot_pos].set(tokens[token_of])
    arrived = lax.all_to_all(send_buf, "ep", split_axis=1, concat_axis=1, tiled=True)
    arrived = arrived.reshape(exp_local, ep_count * capacity, feat_width)
    shard_piece = lax.all_gather(arrived, "tp", axis=2, tiled=True)
    gate_new = jnp.einsum(
        "erd,edf->erf", shard_piece, gate_weight, preferred_element_type=jnp.float32
    )
    up_new = jnp.einsum("erd,edf->erf", shard_piece, up_weight, preferred_element_type=jnp.float32)
    hidden = activate(gate_new, up_new).astype(jnp.bfloat16)
    partials = jnp.einsum("erf,efd->erd", hidden, down_weight, preferred_element_type=jnp.float32)
    weights_flat = combine_weights.reshape(-1)
    summed = lax.psum_scatter(
        partials.astype(jnp.bfloat16), "tp", scatter_dimension=2, tiled=True
    ).astype(jnp.float32)
    summed = summed.reshape(exp_local, ep_count, capacity, summed.shape[2])
    returned = lax.all_to_all(
        summed.astype(jnp.bfloat16), "ep", split_axis=1, concat_axis=1, tiled=True
    ).astype(summed.dtype)
    picked = returned[expert_local, owner_dev, slot_pos]
    weighted = (picked * weights_flat[:, None]).reshape(tok_rows, top_count, picked.shape[1])
    mixed = jnp.sum(weighted, axis=1).astype(jnp.bfloat16)
    return mixed


def solution(mesh):
    in_specs = (
        P("ep", "tp"),
        P("ep", None),
        P("ep", None),
        P("ep", None, "tp"),
        P("ep", None, "tp"),
        P("ep", "tp", None),
    )
    out_specs = P("ep", "tp")
    return jax.shard_map(local, mesh=mesh, in_specs=in_specs, out_specs=out_specs, check_vma=False)
```

profile of v0, /device:TPU:0, one launch (start us, length us, event | category | flops | bytes accessed | tf_op | source)
XLA Modules:
  0.0 439.0 jit_solution(15752584724429517280)
XLA Ops:
  6.5 0.0 all-gather.2.cloned.1.call-start
  6.5 0.8 copy.44
  7.4 0.1 eq.31
  7.5 0.1 eq.27
  7.6 0.1 reshape.209
  7.8 4.5 %reduce-window.6 = s32[16,8,128]{2,1,0:T(8,128)S(1)} reduce-window(s32[16,8,128]{2,1,0:T(8,128)S(1)} %fusion.8, s32[]{:T(128)} %constant.48.clone.1), window={size=1x1x128 pad=0_0x0_0x127_0}, to_apply=%region_0.0 | reduce-window | flops 2080768 | bytes 131076 | tf_op jit(solution)/shard_map/reduce-window
  12.3 0.1 slice.13
  12.4 0.1 copy.47
  12.5 0.1 copy.48
  12.6 0.1 broadcast_add_fusion
  12.7 0.1 shift-left_or_fusion
  12.8 0.7 multiply_reduce_fusion.1
  13.5 0.7 and_reduce_fusion
  14.3 1.2 copy.49
  15.5 12.4 %scatter_custom_fusion = bf16[2048,720]{1,0:T(8,128)(2,1)S(1)} fusion(s32[1024]{0:T(1024)S(1)} %get-tuple-element.10, bf16[256,720]{1,0:T(8,128)(2,1)S(1)} %copy.49, s32[1024]{0:T(1024)S(1)} %get-tuple-element.9, bf16[]{:T(256)} %constant.47.clone.1), kind=kCustom, calls=%fused_computation.10 | custom fusion | bytes 2949122
  27.9 5.5 %copy.51 = bf16[2,8,128,720]{2,0,3,1:T(2,128)(2,1)} copy(bf16[2,8,128,720]{3,2,1,0:T(8,128)(2,1)S(1)} %bitcast.37) | data formatting | bytes 5898240 | tf_op jit(solution)/shard_map/scatter | solution.py:26
  33.5 74.4 %all_to_all.10 = bf16[2,8,128,720]{2,0,3,1:T(2,128)(2,1)S(1)} all-to-all(bf16[2,8,128,720]{2,0,3,1:T(2,128)(2,1)} %copy.51), channel_id=1, replica_groups=mesh['ep'=8,'tp'=4] {'ep'}, dimensions={1} | all-to-all | bytes 5898240 | tf_op jit(solution)/shard_map/all_to_all | solution.py:27
  107.8 1.1 copy.52
  109.0 3.3 reshape.211
  112.2 0.0 all-gather.2.cloned.1.call-update
  112.2 0.2 reduce-scatter.2.cloned.1.call-start
  112.5 76.0 %all-gather.2.cloned.1.call-done = bf16[2,1024,2880]{1,2,0:T(8,128)(2,1)} async-done(((bf16[2,1024,720]{1,2,0:T(8,128)(2,1)}), bf16[2,1024,2880]{1,2,0:T(8,128)(2,1)}) %all-gather.2.cloned.1.call-update) | async-done | bytes 11796496 | tf_op jit(solution)/shard_map/all_gather | solution.py:29
  188.5 16.2 %fusion.13 = f32[2,1024,720]{1,2,0:T(8,128)} fusion(bf16[2,2880,720]{1,2,0:T(8,128)(2,1)} %param.9, bf16[2,1024,2880]{1,2,0:T(8,128)(2,1)} %all-gather.2.cloned.1.call-done), kind=kOutput, calls=%fused_computation.43 | convolution fusion | flops 8493465600 | bytes 25989120 | tf_op jit(solution)/shard_map/erd,edf->erf/dot_general | solution.py:30
  204.6 27.0 %convolution_convert_fusion = bf16[2,1024,2880]{1,2,0:T(8,128)(2,1)} fusion(bf16[2,720,2880]{2,1,0:T(8,128)(2,1)} %param.11, f32[2,1024,720]{1,2,0:T(8,128)} %fusion.13, bf16[2,2880,720]{1,2,0:T(8,128)(2,1)} %param.10, bf16[2,1024,2880]{1,2,0:T(8,128)(2,1)} %all-gather.2.cloned.1.call-done), kind=kOutput, calls=%fused_computation.3 | convolution fusion | flops 17004625920 | bytes 46080000 | tf_op jit(solution)/shard_map/erf,efd->erd/dot_general | solution.py:35
  231.7 0.0 reduce-scatter.2.cloned.1.call-update
  231.7 0.0 copy-start
  231.7 93.6 %reduce-scatter.2.cloned.1.call-done = bf16[2,1024,720]{1,2,0:T(8,128)(2,1)} async-done(((bf16[2,1024,2880]{1,2,0:T(8,128)(2,1)}), bf16[2,1024,720]{1,2,0:T(8,128)(2,1)}) %reduce-scatter.2.cloned.1.call-update) | async-done | bytes 2949136 | tf_op jit(solution)/shard_map/reduce_scatter | solution.py:37
  325.3 4.0 copy_bitcast_fusion
  329.3 5.5 %all-to-all-start.1 = ((bf16[2,8,128,720]{2,3,0,1:T(8,128)(2,1)}), bf16[2,8,128,720]{2,3,0,1:T(8,128)(2,1)S(1)}, u32[]{:S(2)}, u32[]{:S(2)}) async-start(bf16[2,8,128,720]{2,3,0,1:T(8,128)(2,1)} %copy_bitcast_fusion), calls=%async_computation.2 | async-start | bytes 5898240 | tf_op jit(solution)/shard_map/all_to_all | solution.py:41
  334.8 0.0 copy-done
  334.8 0.1 copy.56
  335.0 66.2 %all-to-all-done.1 = bf16[2,8,128,720]{2,3,0,1:T(8,128)(2,1)S(1)} async-done(((bf16[2,8,128,720]{2,3,0,1:T(8,128)(2,1)}), bf16[2,8,128,720]{2,3,0,1:T(8,128)(2,1)S(1)}, u32[]{:S(2)}, u32[]{:S(2)}) %all-to-all-start.1) | async-done | bytes 2949152 | tf_op jit(solution)/shard_map/all_to_all | solution.py:41
  401.1 2.9 copy_convert_fusion
  404.1 6.5 %copy.55 = f32[2,8,128,720]{3,2,1,0:T(8,128)} copy(f32[2,8,128,720]{2,3,1,0:T(8,128)} %copy_convert_fusion) | data formatting | bytes 11796480 | tf_op jit(solution)/shard_map/convert_element_type | solution.py:43
  410.6 14.6 %gather_fusion = f32[1024,720]{1,0:T(8,128)S(1)} fusion(f32[2,8,128,720]{3,2,1,0:T(8,128)} %copy.55, s32[1024]{0:T(1024)S(1)} %bitcast.36), kind=kCustom, calls=%fused_computation.1 | custom fusion | bytes 5910528 | tf_op jit(solution)/shard_map/gather | solution.py:44
  425.2 2.1 gather.10
  427.3 3.9 multiply_reduce_fusion
  431.2 0.9 copy.57
  (6 shorter events, 0.1 us)
Async XLA Ops:
  6.5 181.9 %all-gather.2.cloned.1.call-start = ((), (), s32[]{:S(2)}) async-start(), calls=%async_computation.3 | async-start | bytes 14745600 | tf_op jit(solution)/shard_map/all_gather | solution.py:29
  112.2 213.1 %reduce-scatter.2.cloned.1.call-start = ((), (), s32[]{:S(2)}) async-start(), calls=%async_computation.4 | async-start | bytes 14745600 | tf_op jit(solution)/shard_map/reduce_scatter | solution.py:37
  231.7 103.1 %copy-start = (f32[256,4]{0,1:T(4,128)S(1)}, f32[256,4]{0,1:T(4,128)}, u32[]{:S(2)}) copy-start(f32[256,4]{0,1:T(4,128)} %param.8) | copy-start | bytes 12292
  329.3 71.8 %all-to-all-start.1 = ((bf16[2,8,128,720]{2,3,0,1:T(8,128)(2,1)}), bf16[2,8,128,720]{2,3,0,1:T(8,128)(2,1)S(1)}, u32[]{:S(2)}, u32[]{:S(2)}) async-start(bf16[2,8,128,720]{2,3,0,1:T(8,128)(2,1)} %copy_bitcast_fusion), calls=%async_computation.2 | async-start | bytes 5898240 | tf_op jit(solution)/shard_map/all_to_all | solution.py:41
Sparse Core Ops, SparseCore 0:
  112.4 76.0 all-gather.1
  231.8 93.4 reduce-scatter.1
where the time goes:
time: 440 us; the launch traced here: 439 us
  waiting for transfers between devices  236 us (54%)
  blocking collectives  74.4 us (17%)
  local copies, waits for them, and re-layouts  53.3 us (12%)
  matrix products  43.2 us (10%)
  between operations  13.5 us (3%)
  other arithmetic  13.1 us (3%)
  starting transfers between devices  5.73 us (1%)
    reduce_scatter x1, waiting for transfers between devices, local(): lax.psum_scatter(partials.astype(jnp.bfloat16), 'tp', scatter_dimension=2...  93.6 us
    all_gather x1, waiting for transfers between devices, local(): shard_piece = lax.all_gather(arrived, 'tp', axis=2, tiled=True)  76 us
    all_to_all x1, blocking collectives, local(): lax.all_to_all(send_buf, 'ep', split_axis=1, concat_axis=1, tiled=True)  74.4 us
    all_to_all x1, waiting for transfers between devices, local(): lax.all_to_all(summed.astype(jnp.bfloat16), 'ep', split_axis=1, concat_ax...  66.2 us
    dot_general x1, matrix products, local(): jnp.einsum('erf,efd->erd', hidden, down_weight, preferred_element_type=jn...  27 us
    gather x2, local copies, waits for them, and re-layouts, local(): picked = returned[expert_local, owner_dev, slot_pos]  16.7 us
    dot_general x1, matrix products, local(): jnp.einsum('erd,edf->erf', shard_piece, gate_weight, preferred_element_ty...  16.2 us
    unnamed x6, local copies, waits for them, and re-layouts  14.6 us
  transfers between devices with their start and end apart: 3, of which 3 were waited for; matrix products, arithmetic and copies ran while one was open for 0% of the time, Pallas kernels for 0%

commit v1 on v0

--- a/solution.py
+++ b/solution.py
@@ -24,7 +24,10 @@
     token_of = jnp.arange(tok_rows * top_count, dtype=jnp.int32) // top_count
     send_buf = jnp.zeros((exp_local, ep_count, capacity, feat_width), jnp.bfloat16)
     send_buf = send_buf.at[expert_local, owner_dev, slot_pos].set(tokens[token_of])
-    arrived = lax.all_to_all(send_buf, "ep", split_axis=1, concat_axis=1, tiled=True)
+    arrived = jnp.concatenate(
+        lax.all_to_all(jnp.stack(jnp.split(send_buf, lax.axis_size("ep"), axis=1)), "ep", 0, 0),
+        axis=1,
+    )
     arrived = arrived.reshape(exp_local, ep_count * capacity, feat_width)
     shard_piece = lax.all_gather(arrived, "tp", axis=2, tiled=True)
     gate_new = jnp.einsum(

time: 440 us -> 456 us (1.036)
  local copies, waits for them, and re-layouts: 53.3 us -> 68.9 us
    split x0 -> x9, local copies, waits for them, and re-layouts: none -> 15.8 us  [local(): jnp.split(send_buf, lax.axis_size('ep'), axis=1)]
    scatter x1 -> x0, local copies, waits for them, and re-layouts: 5.54 us -> none  [local(): send_buf.at[expert_local, owner_dev, slot_pos].set(tokens[token_of])]
    unnamed x6 -> x19, local copies, waits for them, and re-layouts: 14.6 us -> 19.9 us
where the time goes in v1:
time: 456 us; the launch traced here: 455 us
  waiting for transfers between devices  236 us (52%)
  blocking collectives  74.2 us (16%)
  local copies, waits for them, and re-layouts  68.9 us (15%)
  matrix products  43.2 us (9%)
  between operations  13.6 us (3%)
  other arithmetic  13.1 us (3%)
  starting transfers between devices  5.86 us (1%)
    reduce_scatter x1, waiting for transfers between devices, local(): lax.psum_scatter(partials.astype(jnp.bfloat16), 'tp', scatter_dimension=2...  93.6 us
    all_gather x1, waiting for transfers between devices, local(): shard_piece = lax.all_gather(arrived, 'tp', axis=2, tiled=True)  76 us
    all_to_all x1, blocking collectives, local(): lax.all_to_all(jnp.stack(jnp.split(send_buf, lax.axis_size('ep'), axis=1)...  74.2 us
    all_to_all x1, waiting for transfers between devices, local(): lax.all_to_all(summed.astype(jnp.bfloat16), 'ep', split_axis=1, concat_ax...  66.2 us
    dot_general x1, matrix products, local(): jnp.einsum('erf,efd->erd', hidden, down_weight, preferred_element_type=jn...  27 us
    unnamed x19, local copies, waits for them, and re-layouts  19.9 us
    gather x2, local copies, waits for them, and re-layouts, local(): picked = returned[expert_local, owner_dev, slot_pos]  16.7 us
    dot_general x1, matrix products, local(): jnp.einsum('erd,edf->erf', shard_piece, gate_weight, preferred_element_ty...  16.2 us
  transfers between devices with their start and end apart: 3, of which 3 were waited for; matrix products, arithmetic and copies ran while one was open for 0% of the time, Pallas kernels for 0%

profile of v1, /device:TPU:0, one launch (start us, length us, event | category | flops | bytes accessed | tf_op | source)
XLA Modules:
  0.0 454.7 jit_solution(16088547828021151776)
XLA Ops:
  6.5 0.8 copy.203
  7.4 0.1 eq.31
  7.5 0.1 eq.27
  7.6 0.1 reshape.209
  7.8 4.5 reduce-window.6
  12.3 0.1 slice.13
  12.4 0.1 copy.206
  12.5 0.1 copy.207
  12.6 0.1 broadcast_add_fusion
  12.7 0.1 shift-left_or_fusion
  12.8 0.7 multiply_reduce_fusion.1
  13.5 0.7 and_reduce_fusion
  14.3 1.2 copy.208
  15.5 12.4 %scatter_custom_fusion = bf16[2048,720]{1,0:T(8,128)(2,1)S(1)} fusion(s32[1024]{0:T(1024)S(1)} %get-tuple-element.18, bf16[256,720]{1,0:T(8,128)(2,1)S(1)} %copy.208, s32[1024]{0:T(1024)S(1)} %get-tuple-element.17, bf16[]{:T(256)} %constant.47.clone.1), kind=kCustom, calls=%fused_computation.10 | custom fusion | bytes 2949122
  27.9 1.6 fusion.13
  29.5 1.9 copy.210
  31.4 1.0 bitcast_dynamic-update-slice_fusion.7
  32.4 1.9 copy.211
  34.3 1.9 copy.212
  36.2 1.9 copy.213
  38.1 1.9 copy.214
  40.0 1.9 copy.215
  42.0 1.9 copy.216
  43.9 0.9 copy.217
  44.8 1.1 bitcast_dynamic-update-slice_fusion.6
  45.9 1.0 bitcast_dynamic-update-slice_fusion.5
  46.9 1.0 bitcast_dynamic-update-slice_fusion.4
  48.0 1.0 bitcast_dynamic-update-slice_fusion.3
  49.0 0.1 bitcast_dynamic-update-slice_fusion.2
  49.2 0.1 bitcast_dynamic-update-slice_fusion
  49.2 74.2 %all_to_all.10 = bf16[8,2,1,128,720]{3,4,2,1,0:T(8,128)(2,1)S(1)} all-to-all(bf16[8,2,1,128,720]{3,4,2,1,0:T(8,128)(2,1)S(1)} %bitcast_dynamic-update-slice_fusion), channel_id=1, replica_groups=mesh['ep'=8,'tp'=4] {'ep'}, dimensions={0} | all-to-all | bytes 5898240 | tf_op jit(solution)/shard_map/all_to_all | solution.py:28
  123.4 1.1 copy.218
  124.5 3.3 reshape_reshape.3
  127.8 0.2 reduce-scatter.2.cloned.1.call-start
  128.0 76.0 %all-gather.2.cloned.1.call-done = bf16[2,1024,2880]{1,2,0:T(8,128)(2,1)} async-done(((bf16[2,1024,720]{1,2,0:T(8,128)(2,1)}), bf16[2,1024,2880]{1,2,0:T(8,128)(2,1)}) %all-gather.2.cloned.1.call-update) | async-done | bytes 11796496 | tf_op jit(solution)/shard_map/all_gather | solution.py:32
  204.0 16.2 %fusion.14 = f32[2,1024,720]{1,2,0:T(8,128)} fusion(bf16[2,2880,720]{1,2,0:T(8,128)(2,1)} %param.9, bf16[2,1024,2880]{1,2,0:T(8,128)(2,1)} %all-gather.2.cloned.1.call-done), kind=kOutput, calls=%fused_computation.52 | convolution fusion | flops 8493465600 | bytes 25989120 | tf_op jit(solution)/shard_map/erd,edf->erf/dot_general | solution.py:33
  220.2 27.0 %convolution_convert_fusion = bf16[2,1024,2880]{1,2,0:T(8,128)(2,1)} fusion(bf16[2,720,2880]{2,1,0:T(8,128)(2,1)} %param.11, f32[2,1024,720]{1,2,0:T(8,128)} %fusion.14, bf16[2,2880,720]{1,2,0:T(8,128)(2,1)} %param.10, bf16[2,1024,2880]{1,2,0:T(8,128)(2,1)} %all-gather.2.cloned.1.call-done), kind=kOutput, calls=%fused_computation.3 | convolution fusion | flops 17004625920 | bytes 46080000 | tf_op jit(solution)/shard_map/erf,efd->erd/dot_general | solution.py:38
  247.3 93.6 %reduce-scatter.2.cloned.1.call-done = bf16[2,1024,720]{1,2,0:T(8,128)(2,1)} async-done(((bf16[2,1024,2880]{1,2,0:T(8,128)(2,1)}), bf16[2,1024,720]{1,2,0:T(8,128)(2,1)}) %reduce-scatter.2.cloned.1.call-update) | async-done | bytes 2949136 | tf_op jit(solution)/shard_map/reduce_scatter | solution.py:40
  340.9 4.0 copy_bitcast_fusion
  344.9 5.6 %all-to-all-start.1 = ((bf16[2,8,128,720]{2,3,0,1:T(8,128)(2,1)}), bf16[2,8,128,720]{2,3,0,1:T(8,128)(2,1)S(1)}, u32[]{:S(2)}, u32[]{:S(2)}) async-start(bf16[2,8,128,720]{2,3,0,1:T(8,128)(2,1)} %copy_bitcast_fusion), calls=%async_computation.2 | async-start | bytes 5898240 | tf_op jit(solution)/shard_map/all_to_all | solution.py:44
  350.5 0.1 copy.222
  350.6 66.2 %all-to-all-done.1 = bf16[2,8,128,720]{2,3,0,1:T(8,128)(2,1)S(1)} async-done(((bf16[2,8,128,720]{2,3,0,1:T(8,128)(2,1)}), bf16[2,8,128,720]{2,3,0,1:T(8,128)(2,1)S(1)}, u32[]{:S(2)}, u32[]{:S(2)}) %all-to-all-start.1) | async-done | bytes 2949152 | tf_op jit(solution)/shard_map/all_to_all | solution.py:44
  416.8 2.9 copy_convert_fusion
  419.8 6.5 %copy.221 = f32[2,8,128,720]{3,2,1,0:T(8,128)} copy(f32[2,8,128,720]{2,3,1,0:T(8,128)} %copy_convert_fusion) | data formatting | bytes 11796480 | tf_op jit(solution)/shard_map/convert_element_type | solution.py:46
  426.2 14.6 %gather_fusion = f32[1024,720]{1,0:T(8,128)S(1)} fusion(f32[2,8,128,720]{3,2,1,0:T(8,128)} %copy.221, s32[1024]{0:T(1024)S(1)} %bitcast.53), kind=kCustom, calls=%fused_computation.1 | custom fusion | bytes 5910528 | tf_op jit(solution)/shard_map/gather | solution.py:47
  440.8 2.2 gather.10
  443.0 3.9 multiply_reduce_fusion
  446.9 0.9 copy.223
  (18 shorter events, 0.2 us)
Async XLA Ops:
  6.5 197.5 %all-gather.2.cloned.1.call-start = ((), (), s32[]{:S(2)}) async-start(), calls=%async_computation.3 | async-start | bytes 14745600 | tf_op jit(solution)/shard_map/all_gather | solution.py:32
  44.8 4.3 copy-start.2
  44.8 4.3 copy-start
  44.8 4.4 copy-start.1
  127.8 213.1 %reduce-scatter.2.cloned.1.call-start = ((), (), s32[]{:S(2)}) async-start(), calls=%async_computation.4 | async-start | bytes 14745600 | tf_op jit(solution)/shard_map/reduce_scatter | solution.py:40
  344.9 5.6 %copy-start.3 = (f32[256,4]{0,1:T(4,128)S(1)}, f32[256,4]{0,1:T(4,128)}, u32[]{:S(2)}) copy-start(f32[256,4]{0,1:T(4,128)} %param.8) | copy-start | bytes 12292
  344.9 72.0 %all-to-all-start.1 = ((bf16[2,8,128,720]{2,3,0,1:T(8,128)(2,1)}), bf16[2,8,128,720]{2,3,0,1:T(8,128)(2,1)S(1)}, u32[]{:S(2)}, u32[]{:S(2)}) async-start(bf16[2,8,128,720]{2,3,0,1:T(8,128)(2,1)} %copy_bitcast_fusion), calls=%async_computation.2 | async-start | bytes 5898240 | tf_op jit(solution)/shard_map/all_to_all | solution.py:44
Sparse Core Ops, SparseCore 0:
  127.9 76.0 all-gather.1
  247.4 93.4 reduce-scatter.1
